TPU v7x, 32 devices: a whole 2x2x4 slice. The times are simulated.
32 devices in a mesh: grp: 2 (over y), hist: 4 (over z), chan: 2 (over x), seq: 2 (over core).
Axes of the slice: x: 2, y: 2, z: 4, core: 2. Of those that a mesh axis runs over, the one named last changes fastest.
Arguments:
- history: bfloat16 [16, 2048, 4096], P(('grp', 'seq'), 'hist', 'chan'), parts along dimension 0, may hold values from -6 to 6
- filter_taps: bfloat16 [4096, 4096], P(('grp', 'hist'), 'chan'), parts along dimension 0, may hold values from -0.125 to 0.125
- skip_gain: float32 [8192], P(('grp', 'chan')), parts along dimension 0, may hold values from -4 to 4
- gate_values: bfloat16 [16, 64, 4096], P(('grp', 'seq'), 'hist', 'chan'), parts along dimension 0, may hold values from -6 to 6
Outputs:
- output: bfloat16 [16, 64, 4096], P(('grp', 'seq'), 'hist', 'chan'), parts along dimension 0
There are 2 independent parts, one for each index of `grp`. A program takes and returns all parts, laid end to end along the dimension named above; each array names one. Nothing has to cross between parts.
All inputs are finite; a program needn't handle non-finite values.
Results may differ from a plain program's by a relative error of at most 0.0085.
Values may be sent and summed in bfloat16 or wider, within the bound.
A program may use at most 192 MiB of HBM per device.

v0:
```python
import functools
import math

import jax
import jax.numpy as jnp
import numpy as np
from jax import lax
from jax.experimental import pallas as pl
from jax.experimental.pallas import tpu as pltpu
from jax.sharding import PartitionSpec as P

MESH = pl.DeviceIdType.MESH
F32 = jnp.float32
BF16 = jnp.bfloat16
LAG = 2
GAP = 4
DEPTH = 2


def tables(new, piece):
    length = piece + new
    freqs = 2 * np.arange(length // 2)[:, None] + 1

    def both(times):
        angle = math.pi / length * (freqs * times[None, :] % (2 * length))
        pairs = np.stack([np.cos(angle), np.sin(angle)]).reshape(2, -1, 16, times.size)
        return pairs.transpose(1, 0, 2, 3).reshape(length, times.size)

    taps_table = both(np.arange(length))
    data_table = both(np.arange(piece))
    back_table = both(new - 1 - np.arange(new)).T * (2.0 / length)
    return [jnp.asarray(table, BF16) for table in (taps_table, data_table, back_table)]


def kernel(
    n, new, piece, width,
    ft_hbm, fh_hbm, fi_hbm, hist_hbm, taps_hbm, gain_hbm, gate_hbm, out_hbm,
    ft, fh, fi, hist, taps, gain, gate, out, tspec, dspec, spec, part,
    send, recv, in_sem, small_sem, out_sem, rim_sem, pass_sem, open_sem, send_sem, recv_sem,
):
    me = lax.axis_index("hist")
    core, cores = lax.axis_index("seq"), lax.axis_size("seq")
    right, left = me + 1, me - 1
    first, last = me == 0, me == n - 1
    chunks, seqs, block, _ = hist.shape
    own = new // n
    bins = (piece + new) // 2
    pieces = block // piece
    direct = chunks // cores
    ends = n - 1 - me

    def lanes(i):
        c = lax.rem(i + core * direct, chunks)
        return pl.ds(pl.multiple_of(c * width, width), width)

    small = [
        pltpu.make_async_copy(source, target, small_sem.at[i])
        for i, (source, target) in enumerate(
            [(ft_hbm, ft), (fh_hbm, fh), (fi_hbm, fi), (gain_hbm, gain), (gate_hbm, gate)]
        )
    ]

    def load_taps(i):
        return pltpu.make_async_copy(
            taps_hbm.at[:, lanes(i)], taps.at[i, pl.ds(0, block)], in_sem.at[0, i]
        )

    def load_hist(i):
        return pltpu.make_async_copy(hist_hbm.at[:, :, lanes(i)], hist.at[i], in_sem.at[1, i])

    def store(i):
        return pltpu.make_async_copy(out.at[i], out_hbm.at[:, :, lanes(i)], out_sem.at[i])

    def rim_copy(i):
        return pltpu.make_async_remote_copy(
            src_ref=taps_hbm.at[pl.ds(0, new), lanes(i)],
            dst_ref=taps.at[i, pl.ds(block, new)],
            send_sem=rim_sem.at[0, i],
            recv_sem=rim_sem.at[1, i],
            device_id={"hist": left},
            device_id_type=MESH,
        )

    def rim_pass(i, far):
        j = i + far * direct
        return pltpu.make_async_remote_copy(
            src_ref=taps.at[i, pl.ds(block, new)],
            dst_ref=taps.at[j, pl.ds(block, new)],
            send_sem=pass_sem.at[far - 1, i],
            recv_sem=rim_sem.at[1, j],
            device_id={"seq": lax.rem(core + cores - far, cores)},
            device_id_type=MESH,
        )

    def hop(way, owner, i):
        return pltpu.make_async_remote_copy(
            src_ref=send.at[way, owner, i],
            dst_ref=recv.at[way, owner, i],
            send_sem=send_sem.at[way, owner, i],
            recv_sem=recv_sem.at[way, owner, i],
            device_id={"hist": right if way == 0 else left},
            device_id_type=MESH,
        )

    for copy in small[:3]:
        copy.start()

    def start_loads(i, carry):
        load_taps(i).start()
        load_hist(i).start()
        return carry

    lax.fori_loop(0, min(DEPTH, chunks), start_loads, 0)
    for copy in small[3:]:
        copy.start()

    barrier = pltpu.get_barrier_semaphore()

    @pl.when(jnp.logical_not(last))
    def _():
        pl.semaphore_signal(barrier, inc=1, device_id={"hist": right}, device_id_type=MESH)

    for far in range(1, cores):
        pl.semaphore_signal(
            barrier, inc=1, device_id={"seq": lax.rem(core + far, cores)}, device_id_type=MESH
        )
    pl.semaphore_wait(barrier, cores - first.astype(jnp.int32))

    def start_rims(i, carry):
        rim_copy(i).start()
        return carry

    @pl.when(jnp.logical_not(first))
    def _():
        pl.semaphore_signal(open_sem, inc=1, device_id={"hist": left}, device_id_type=MESH)
        lax.fori_loop(0, direct, start_rims, 0)

    for copy in small:
        copy.wait()
    latest = last.astype(F32)

    def arrive(i):
        @pl.when(i + DEPTH < chunks)
        def _():
            start_loads(i + DEPTH, 0)

        load_taps(i).wait()
        load_hist(i).wait()

    def arrive_rim(i):
        @pl.when(jnp.logical_not(last))
        def _():
            rim_copy(i).wait_recv()

            @pl.when(i < direct)
            def _():
                for far in range(1, cores):
                    rim_pass(i, far).start()

        @pl.when(last)
        def _():
            taps[i, pl.ds(block, new)] = jnp.zeros((new, width), BF16)

    def transform(i, b, slot):
        for q in range(pieces):
            dspec[slot, b, q] = jnp.dot(
                fh[...], hist[i, b, pl.ds(q * piece, piece)], preferred_element_type=F32
            )

    def transform_taps(i, q, slot):
        tspec[slot, q] = jnp.dot(
            ft[...], taps[i, pl.ds(q * piece, piece + new)], preferred_element_type=F32
        )

    def compute(i, slot):
        gains = gain[:, lanes(i)] * latest
        ahead = jnp.minimum(i + 1, chunks - 1)
        for b in range(max(seqs, pieces)):
            if b < seqs:
                transform(ahead, b, 1 - slot)
            if b < pieces:
                transform_taps(ahead, b, 1 - slot)
            if b >= seqs:
                continue
            for r in range(0, bins, 16):
                low, high = pl.ds(2 * r, 16), pl.ds(2 * r + 16, 16)
                real = imag = None
                for q in range(pieces):
                    hc, hs = dspec[slot, b, q, low], dspec[slot, b, q, high]
                    tc, ts = tspec[slot, q, low], tspec[slot, q, high]
                    one, two = tc * hc + ts * hs, ts * hc - tc * hs
                    real = one if q == 0 else real + one
                    imag = two if q == 0 else imag + two
                spec[b, low] = real.astype(BF16)
                spec[b, high] = imag.astype(BF16)
            value = jnp.dot(fi[...], spec[b], preferred_element_type=F32)
            value = value + gains * hist[i, b, pl.ds(block - new, new)].astype(F32)
            for d in range(n):
                part[i, d, b] = value[d * own : (d + 1) * own]

    def pass_on(way, owner, i):
        edge = first if way == 0 else last

        @pl.when(edge)
        def _():
            for b in range(seqs):
                send[way, owner, i, b] = part[i, owner, b].astype(BF16)

        @pl.when(jnp.logical_not(edge))
        def _():
            hop(way, owner, i).wait_recv()
            for b in range(seqs):
                value = part[i, owner, b] + recv[way, owner, i, b].astype(F32)
                send[way, owner, i, b] = value.astype(BF16)

        hop(way, owner, i).start()

    def finish(i):
        @pl.when(jnp.logical_not(first))
        def _():
            hop(0, me, i).wait_recv()
            for b in range(seqs):
                part[i, me, b] += recv[0, me, i, b].astype(F32)

        @pl.when(jnp.logical_not(last))
        def _():
            hop(1, me, i).wait_recv()
            for b in range(seqs):
                part[i, me, b] += recv[1, me, i, b].astype(F32)

        for b in range(seqs):
            out_hbm[b, :, lanes(i)] = (gate[b, :, lanes(i)].astype(F32) * part[i, me, b]).astype(BF16)

    def guarded(i, action):
        @pl.when(jnp.logical_and(i >= 0, i < chunks))
        def _():
            action(i)

    def turn(k):
        return GAP * k + jnp.where(k == n - 2, chunks - GAP, 0)

    final = jnp.where(
        jnp.logical_or(first, last),
        chunks + turn(n - 2),
        jnp.maximum(LAG * ends + turn(me), LAG * me + turn(ends)),
    )

    def step(t, slot):
        @pl.when(t + 1 < chunks)
        def _():
            arrive(t + 1)
            arrive_rim(t + 1)

        @pl.when(t < chunks)
        def _():
            compute(t, slot)

        def to_left(k, carry):
            guarded(t - LAG * ends - turn(k), functools.partial(pass_on, 1, k))
            return carry

        def to_right(k, carry):
            guarded(t - LAG * me - turn(k), functools.partial(pass_on, 0, n - 1 - k))
            return carry

        lax.fori_loop(0, me, to_left, 0)
        lax.fori_loop(0, ends, to_right, 0)
        guarded(t - final, finish)

    def steps(p, carry):
        for slot in range(2):
            step(2 * p + slot, slot)
        return carry

    arrive(0)
    for b in range(seqs):
        transform(0, b, 0)
    arrive_rim(0)
    for q in range(pieces):
        transform_taps(0, q, 0)

    @pl.when(jnp.logical_not(last))
    def _():
        pl.semaphore_wait(open_sem, 1)

    lax.fori_loop(0, (chunks + final + 1) // 2, steps, 0)

    def drain(i, carry):

        @pl.when(jnp.logical_and(i < direct, jnp.logical_not(first)))
        def _():
            rim_copy(i).wait_send()

        @pl.when(jnp.logical_and(i < direct, jnp.logical_not(last)))
        def _():
            for far in range(1, cores):
                rim_pass(i, far).wait_send()

        def drain_left(k, carry):
            hop(1, k, i).wait_send()
            return carry

        def drain_right(k, carry):
            hop(0, n - 1 - k, i).wait_send()
            return carry

        lax.fori_loop(0, me, drain_left, 0)
        lax.fori_loop(0, ends, drain_right, 0)
        return carry

    lax.fori_loop(0, chunks, drain, 0)


def body(history, filter_taps, skip_gain, gate_values):
    n = lax.axis_size("hist")
    seqs, block, channels = history.shape
    own = gate_values.shape[1]
    new = own * n
    piece = min(2 * new, block)
    width = min(256, channels)
    chunks = channels // width
    length = piece + new
    cores = lax.axis_size("seq")
    hbm = pl.BlockSpec(memory_space=pl.ANY)
    return pl.pallas_call(
        functools.partial(kernel, n, new, piece, width),
        out_shape=pltpu.VMEM(gate_values.shape, BF16),
        in_specs=[hbm] * 7,
        out_specs=pl.BlockSpec(memory_space=pltpu.VMEM),
        scratch_shapes=[
            pltpu.VMEM((length, length), BF16),
            pltpu.VMEM((length, piece), BF16),
            pltpu.VMEM((new, length), BF16),
            pltpu.VMEM((chunks, seqs, block, width), BF16),
            pltpu.VMEM((chunks, block + new, width), BF16),
            pltpu.VMEM((1, channels), F32),
            pltpu.VMEM(gate_values.shape, BF16),
            pltpu.VMEM((chunks, seqs, own, width), BF16),
            pltpu.VMEM((2, block // piece, length, width), F32),
            pltpu.VMEM((2, seqs, block // piece, length, width), F32),
            pltpu.VMEM((seqs, length, width), BF16),
            pltpu.VMEM((chunks, n, seqs, own, width), F32),
            pltpu.VMEM((2, n, chunks, seqs, own, width), BF16),
            pltpu.VMEM((2, n, chunks, seqs, own, width), BF16),
            pltpu.SemaphoreType.DMA((2, chunks)),
            pltpu.SemaphoreType.DMA((5,)),
            pltpu.SemaphoreType.DMA((chunks,)),
            pltpu.SemaphoreType.DMA((2, chunks)),
            pltpu.SemaphoreType.DMA((max(cores - 1, 1), chunks // cores)),
            pltpu.SemaphoreType.REGULAR,
            pltpu.SemaphoreType.DMA((2, n, chunks)),
            pltpu.SemaphoreType.DMA((2, n, chunks)),
        ],
        compiler_params=pltpu.CompilerParams(
            collective_id=0, has_side_effects=True, vmem_limit_bytes=60 * 2**20
        ),
    )(*tables(new, piece), history, filter_taps, skip_gain[None, :], gate_values)


def solution(mesh):
    placed = (
        P(("grp", "seq"), "hist", "chan"),
        P(("grp", "hist"), "chan"),
        P(("grp", "chan")),
        P(("grp", "seq"), "hist", "chan"),
    )
    return jax.shard_map(
        body,
        mesh=mesh,
        in_specs=placed,
        out_specs=P(("grp", "seq"), "hist", "chan"),
        check_vma=False,
    )
```

profile of v0, /device:TPU:0, one launch (start us, length us, event | category | flops | bytes accessed | tf_op | source)
XLA Modules:
  0.0 29.0 jit_solution(6080037314353990525)
XLA Ops:
  0.0 28.3 %shard_map.73 = bf16[4,16,2048]{2,1,0:T(8,128)(2,1)S(1)} custom-call(bf16[192,192]{1,0:T(8,128)(2,1)} %constant.6.clone.ft_hbm, bf16[192,128]{1,0:T(8,128)(2,1)} %constant.7.clone.fh_hbm, bf16[64,192]{1,0:T(8,128)(2,1)} %constant.8.clone.fi_hbm, bf16[4,512,2048]{2,1,0:T(8,128)(2,1)} %hist_hbm.1, bf16[512,2048]{1,0:T(8,128)(2,1)} %taps_hbm.1, ...), custom_call_target="tpu_custom_call" | custom-call | tf_op jit(solution)/shard_map/pallas_call | solution.py:325
  28.3 0.7 %copy.9 = bf16[4,16,2048]{2,1,0:T(8,128)(2,1)} copy(bf16[4,16,2048]{2,1,0:T(8,128)(2,1)S(1)} %shard_map.73) | data formatting | bytes 524288
where the time goes:
time: 29.1 us; the launch traced here: 29 us
  Pallas kernels  28.3 us (97%)
  local copies, waits for them, and re-layouts  0.71 us (2%)
    pallas_call x1, Pallas kernels, body(): pl.pallas_call(functools.partial(kernel, n, new, piece, width), out_shape...  28.3 us
    unnamed x1, local copies, waits for them, and re-layouts  0.71 us

commit v1 on v0

--- a/solution.py
+++ b/solution.py
@@ -12,8 +12,9 @@
 MESH = pl.DeviceIdType.MESH
 F32 = jnp.float32
 BF16 = jnp.bfloat16
-LAG = 2
-GAP = 4
+HOP = 3
+LEFT_GAP = 5
+RIGHT_GAP = 2
 DEPTH = 2
 
 
@@ -34,9 +35,9 @@
 
 def kernel(
     n, new, piece, width,
-    ft_hbm, fh_hbm, fi_hbm, hist_hbm, taps_hbm, gain_hbm, gate_hbm, out_hbm,
-    ft, fh, fi, hist, taps, gain, gate, out, tspec, dspec, spec, part,
-    send, recv, in_sem, small_sem, out_sem, rim_sem, pass_sem, open_sem, send_sem, recv_sem,
+    ft_hbm, fh_hbm, fi_hbm, hist_hbm, taps_hbm, gain_hbm, gate_hbm, total,
+    ft, fh, fi, hist, taps, gain, gate, tspec, dspec, spec, part,
+    send, recv, in_sem, small_sem, rim_sem, pass_sem, open_sem, send_sem, recv_sem,
 ):
     me = lax.axis_index("hist")
     core, cores = lax.axis_index("seq"), lax.axis_size("seq")
@@ -62,43 +63,68 @@
 
     def load_taps(i):
         return pltpu.make_async_copy(
-            taps_hbm.at[:, lanes(i)], taps.at[i, pl.ds(0, block)], in_sem.at[0, i]
+            taps_hbm.at[:, lanes(i)],
+            taps.at[i, pl.ds(0, block)],
+            in_sem.at[0, lax.rem(i, DEPTH + 1)],
         )
 
     def load_hist(i):
-        return pltpu.make_async_copy(hist_hbm.at[:, :, lanes(i)], hist.at[i], in_sem.at[1, i])
-
-    def store(i):
-        return pltpu.make_async_copy(out.at[i], out_hbm.at[:, :, lanes(i)], out_sem.at[i])
-
-    def rim_copy(i):
+        return pltpu.make_async_copy(
+            hist_hbm.at[:, :, lanes(i)], hist.at[i], in_sem.at[1, lax.rem(i, DEPTH + 1)]
+        )
+
+    def rim(source, target, i):
         return pltpu.make_async_remote_copy(
-            src_ref=taps_hbm.at[pl.ds(0, new), lanes(i)],
-            dst_ref=taps.at[i, pl.ds(block, new)],
-            send_sem=rim_sem.at[0, i],
-            recv_sem=rim_sem.at[1, i],
+            src_ref=source,
+            dst_ref=target,
+            send_sem=pass_sem.at[0],
+            recv_sem=rim_sem.at[i],
             device_id={"hist": left},
             device_id_type=MESH,
         )
+
+    def rim_copy(i):
+        return rim(taps_hbm.at[pl.ds(0, new), lanes(i)], taps.at[i, pl.ds(block, new)], i)
 
     def rim_pass(i, far):
         j = i + far * direct
         return pltpu.make_async_remote_copy(
             src_ref=taps.at[i, pl.ds(block, new)],
             dst_ref=taps.at[j, pl.ds(block, new)],
-            send_sem=pass_sem.at[far - 1, i],
-            recv_sem=rim_sem.at[1, j],
+            send_sem=pass_sem.at[far],
+            recv_sem=rim_sem.at[j],
             device_id={"seq": lax.rem(core + cores - far, cores)},
             device_id_type=MESH,
         )
 
+    def all_passed(far):
+        rims = taps.at[pl.ds(0, direct), pl.ds(block, new)]
+        return pltpu.make_async_remote_copy(
+            src_ref=rims,
+            dst_ref=rims,
+            send_sem=pass_sem.at[far],
+            recv_sem=rim_sem.at[0],
+            device_id={"hist": left},
+            device_id_type=MESH,
+        )
+
     def hop(way, owner, i):
         return pltpu.make_async_remote_copy(
-            src_ref=send.at[way, owner, i],
-            dst_ref=recv.at[way, owner, i],
-            send_sem=send_sem.at[way, owner, i],
-            recv_sem=recv_sem.at[way, owner, i],
+            src_ref=send.at[owner, i],
+            dst_ref=recv.at[owner + 1 - way, i],
+            send_sem=send_sem.at[owner],
+            recv_sem=recv_sem.at[owner + 1 - way, i],
             device_id={"hist": right if way == 0 else left},
+            device_id_type=MESH,
+        )
+
+    def all_sent(owner):
+        return pltpu.make_async_remote_copy(
+            src_ref=send.at[owner],
+            dst_ref=recv.at[owner],
+            send_sem=send_sem.at[owner],
+            recv_sem=recv_sem.at[owner, 0],
+            device_id={"hist": right},
             device_id_type=MESH,
         )
 
@@ -120,11 +146,16 @@
     def _():
         pl.semaphore_signal(barrier, inc=1, device_id={"hist": right}, device_id_type=MESH)
 
-    for far in range(1, cores):
-        pl.semaphore_signal(
-            barrier, inc=1, device_id={"seq": lax.rem(core + far, cores)}, device_id_type=MESH
-        )
-    pl.semaphore_wait(barrier, cores - first.astype(jnp.int32))
+    for other in range(1, cores):
+        @pl.when(core < other)
+        def _():
+            pl.semaphore_signal(barrier, inc=1, device_id={"seq": other}, device_id_type=MESH)
+
+    greeted = core + 1 - first.astype(jnp.int32)
+
+    @pl.when(greeted > 0)
+    def _():
+        pl.semaphore_wait(barrier, greeted)
 
     def start_rims(i, carry):
         rim_copy(i).start()
@@ -132,8 +163,15 @@
 
     @pl.when(jnp.logical_not(first))
     def _():
-        pl.semaphore_signal(open_sem, inc=1, device_id={"hist": left}, device_id_type=MESH)
+        pl.semaphore_signal(open_sem.at[0], inc=1, device_id={"hist": left}, device_id_type=MESH)
         lax.fori_loop(0, direct, start_rims, 0)
+
+    for other in range(cores - 1):
+        @pl.when(core > other)
+        def _():
+            pl.semaphore_signal(
+                open_sem.at[1], inc=1, device_id={"seq": other}, device_id_type=MESH
+            )
 
     for copy in small:
         copy.wait()
@@ -204,14 +242,14 @@
         @pl.when(edge)
         def _():
             for b in range(seqs):
-                send[way, owner, i, b] = part[i, owner, b].astype(BF16)
+                send[owner, i, b] = part[i, owner, b].astype(BF16)
 
         @pl.when(jnp.logical_not(edge))
         def _():
             hop(way, owner, i).wait_recv()
             for b in range(seqs):
-                value = part[i, owner, b] + recv[way, owner, i, b].astype(F32)
-                send[way, owner, i, b] = value.astype(BF16)
+                value = part[i, owner, b] + recv[owner + 1 - way, i, b].astype(F32)
+                send[owner, i, b] = value.astype(BF16)
 
         hop(way, owner, i).start()
 
@@ -220,29 +258,32 @@
         def _():
             hop(0, me, i).wait_recv()
             for b in range(seqs):
-                part[i, me, b] += recv[0, me, i, b].astype(F32)
+                part[i, me, b] += recv[me + 1, i, b].astype(F32)
 
         @pl.when(jnp.logical_not(last))
         def _():
             hop(1, me, i).wait_recv()
             for b in range(seqs):
-                part[i, me, b] += recv[1, me, i, b].astype(F32)
+                part[i, me, b] += recv[me, i, b].astype(F32)
 
         for b in range(seqs):
-            out_hbm[b, :, lanes(i)] = (gate[b, :, lanes(i)].astype(F32) * part[i, me, b]).astype(BF16)
+            total[b, :, lanes(i)] = (gate[b, :, lanes(i)].astype(F32) * part[i, me, b]).astype(BF16)
 
     def guarded(i, action):
         @pl.when(jnp.logical_and(i >= 0, i < chunks))
         def _():
             action(i)
 
-    def turn(k):
-        return GAP * k + jnp.where(k == n - 2, chunks - GAP, 0)
-
+    def turn(way, k):
+        gap = RIGHT_GAP if way == 0 else LEFT_GAP
+        return gap * k + jnp.where(k == n - 2, chunks - gap, 0)
+
+    left_lag = jnp.where(last, 0, HOP * ends - 1)
+    right_lag = jnp.where(first, 0, HOP * me + 1)
     final = jnp.where(
         jnp.logical_or(first, last),
-        chunks + turn(n - 2),
-        jnp.maximum(LAG * ends + turn(me), LAG * me + turn(ends)),
+        jnp.maximum(chunks + jnp.maximum(turn(0, n - 2), turn(1, n - 2)), HOP * n),
+        jnp.maximum(left_lag + turn(1, me), right_lag + turn(0, ends)),
     )
 
     def step(t, slot):
@@ -256,11 +297,11 @@
             compute(t, slot)
 
         def to_left(k, carry):
-            guarded(t - LAG * ends - turn(k), functools.partial(pass_on, 1, k))
+            guarded(t - left_lag - turn(1, k), functools.partial(pass_on, 1, k))
             return carry
 
         def to_right(k, carry):
-            guarded(t - LAG * me - turn(k), functools.partial(pass_on, 0, n - 1 - k))
+            guarded(t - right_lag - turn(0, k), functools.partial(pass_on, 0, n - 1 - k))
             return carry
 
         lax.fori_loop(0, me, to_left, 0)
@@ -275,40 +316,39 @@
     arrive(0)
     for b in range(seqs):
         transform(0, b, 0)
+    for q in range(pieces - 1):
+        transform_taps(0, q, 0)
+
+    @pl.when(core < cores - 1)
+    def _():
+        pl.semaphore_wait(open_sem.at[1], cores - 1 - core)
+
     arrive_rim(0)
-    for q in range(pieces):
-        transform_taps(0, q, 0)
+    transform_taps(0, pieces - 1, 0)
 
     @pl.when(jnp.logical_not(last))
     def _():
-        pl.semaphore_wait(open_sem, 1)
+        pl.semaphore_wait(open_sem.at[0], 1)
 
     lax.fori_loop(0, (chunks + final + 1) // 2, steps, 0)
 
-    def drain(i, carry):
-
-        @pl.when(jnp.logical_and(i < direct, jnp.logical_not(first)))
-        def _():
-            rim_copy(i).wait_send()
-
-        @pl.when(jnp.logical_and(i < direct, jnp.logical_not(last)))
-        def _():
-            for far in range(1, cores):
-                rim_pass(i, far).wait_send()
-
-        def drain_left(k, carry):
-            hop(1, k, i).wait_send()
-            return carry
-
-        def drain_right(k, carry):
-            hop(0, n - 1 - k, i).wait_send()
-            return carry
-
-        lax.fori_loop(0, me, drain_left, 0)
-        lax.fori_loop(0, ends, drain_right, 0)
+    @pl.when(jnp.logical_not(first))
+    def _():
+        all_passed(0).wait_send()
+
+    @pl.when(jnp.logical_not(last))
+    def _():
+        for far in range(1, cores):
+            all_passed(far).wait_send()
+
+    def drain(owner, carry):
+        @pl.when(owner != me)
+        def _():
+            all_sent(owner).wait_send()
+
         return carry
 
-    lax.fori_loop(0, chunks, drain, 0)
+    lax.fori_loop(0, n, drain, 0)
 
 
 def body(history, filter_taps, skip_gain, gate_values):
@@ -335,21 +375,19 @@
             pltpu.VMEM((chunks, block + new, width), BF16),
             pltpu.VMEM((1, channels), F32),
             pltpu.VMEM(gate_values.shape, BF16),
-            pltpu.VMEM((chunks, seqs, own, width), BF16),
             pltpu.VMEM((2, block // piece, length, width), F32),
             pltpu.VMEM((2, seqs, block // piece, length, width), F32),
             pltpu.VMEM((seqs, length, width), BF16),
             pltpu.VMEM((chunks, n, seqs, own, width), F32),
-            pltpu.VMEM((2, n, chunks, seqs, own, width), BF16),
-            pltpu.VMEM((2, n, chunks, seqs, own, width), BF16),
-            pltpu.SemaphoreType.DMA((2, chunks)),
+            pltpu.VMEM((n, chunks, seqs, own, width), BF16),
+            pltpu.VMEM((n + 1, chunks, seqs, own, width), BF16),
+            pltpu.SemaphoreType.DMA((2, DEPTH + 1)),
             pltpu.SemaphoreType.DMA((5,)),
             pltpu.SemaphoreType.DMA((chunks,)),
-            pltpu.SemaphoreType.DMA((2, chunks)),
-            pltpu.SemaphoreType.DMA((max(cores - 1, 1), chunks // cores)),
-            pltpu.SemaphoreType.REGULAR,
-            pltpu.SemaphoreType.DMA((2, n, chunks)),
-            pltpu.SemaphoreType.DMA((2, n, chunks)),
+            pltpu.SemaphoreType.DMA((cores,)),
+            pltpu.SemaphoreType.REGULAR((2,)),
+            pltpu.SemaphoreType.DMA((n,)),
+            pltpu.SemaphoreType.DMA((n + 1, chunks)),
         ],
         compiler_params=pltpu.CompilerParams(
             collective_id=0, has_side_effects=True, vmem_limit_bytes=60 * 2**20

time: 29.1 us -> 26.3 us (0.904)
  Pallas kernels: 28.3 us -> 25.5 us
    pallas_call x1, Pallas kernels: 28.3 us -> 25.5 us  [body(): pl.pallas_call(functools.partial(kernel, n, new, piece, width), out_shape...]
where the time goes in v1:
time: 26.3 us; the launch traced here: 26.2 us
  Pallas kernels  25.5 us (97%)
  local copies, waits for them, and re-layouts  0.71 us (3%)
    pallas_call x1, Pallas kernels, body(): pl.pallas_call(functools.partial(kernel, n, new, piece, width), out_shape...  25.5 us
    unnamed x1, local copies, waits for them, and re-layouts  0.71 us

profile of v1, /device:TPU:0, one launch (start us, length us, event | category | flops | bytes accessed | tf_op | source)
XLA Modules:
  0.0 26.2 jit_solution(4169137629972441717)
XLA Ops:
  0.0 25.5 %shard_map.73 = bf16[4,16,2048]{2,1,0:T(8,128)(2,1)S(1)} custom-call(bf16[192,192]{1,0:T(8,128)(2,1)} %constant.6.clone.ft_hbm, bf16[192,128]{1,0:T(8,128)(2,1)} %constant.7.clone.fh_hbm, bf16[64,192]{1,0:T(8,128)(2,1)} %constant.8.clone.fi_hbm, bf16[4,512,2048]{2,1,0:T(8,128)(2,1)} %hist_hbm.1, bf16[512,2048]{1,0:T(8,128)(2,1)} %taps_hbm.1, ...), custom_call_target="tpu_custom_call" | custom-call | tf_op jit(solution)/shard_map/pallas_call | solution.py:365
  25.5 0.7 %copy.9 = bf16[4,16,2048]{2,1,0:T(8,128)(2,1)} copy(bf16[4,16,2048]{2,1,0:T(8,128)(2,1)S(1)} %shard_map.73) | data formatting | bytes 524288

commit v2 on v1

--- a/solution.py
+++ b/solution.py
@@ -12,9 +12,10 @@
 MESH = pl.DeviceIdType.MESH
 F32 = jnp.float32
 BF16 = jnp.bfloat16
-HOP = 3
+LEFT_HOP = 3
 LEFT_GAP = 5
-RIGHT_GAP = 2
+RIGHT_GAP = 0
+RIGHT_HOP = 4
 DEPTH = 2
 
 
@@ -278,11 +279,11 @@
         gap = RIGHT_GAP if way == 0 else LEFT_GAP
         return gap * k + jnp.where(k == n - 2, chunks - gap, 0)
 
-    left_lag = jnp.where(last, 0, HOP * ends - 1)
-    right_lag = jnp.where(first, 0, HOP * me + 1)
+    left_lag = jnp.where(last, 0, LEFT_HOP * ends - 1)
+    right_lag = jnp.where(first, 0, RIGHT_HOP * me)
     final = jnp.where(
         jnp.logical_or(first, last),
-        jnp.maximum(chunks + jnp.maximum(turn(0, n - 2), turn(1, n - 2)), HOP * n),
+        jnp.maximum(chunks + jnp.maximum(turn(0, n - 2), turn(1, n - 2)), max(LEFT_HOP, RIGHT_HOP) * n),
         jnp.maximum(left_lag + turn(1, me), right_lag + turn(0, ends)),
     )
 

time: 26.3 us -> 25.8 us (0.981)
  Pallas kernels: 25.5 us -> 24.9 us
    pallas_call x1, Pallas kernels: 25.5 us -> 24.9 us  [body(): pl.pallas_call(functools.partial(kernel, n, new, piece, width), out_shape...]
where the time goes in v2:
time: 25.8 us; the launch traced here: 25.6 us
  Pallas kernels  24.9 us (97%)
  local copies, waits for them, and re-layouts  0.71 us (3%)
    pallas_call x1, Pallas kernels, body(): pl.pallas_call(functools.partial(kernel, n, new, piece, width), out_shape...  24.9 us
    unnamed x1, local copies, waits for them, and re-layouts  0.71 us

profile of v2, /device:TPU:0, one launch (start us, length us, event | category | flops | bytes accessed | tf_op | source)
XLA Modules:
  0.0 25.6 jit_solution(9851641660208374563)
XLA Ops:
  0.0 24.9 %shard_map.73 = bf16[4,16,2048]{2,1,0:T(8,128)(2,1)S(1)} custom-call(bf16[192,192]{1,0:T(8,128)(2,1)} %constant.6.clone.ft_hbm, bf16[192,128]{1,0:T(8,128)(2,1)} %constant.7.clone.fh_hbm, bf16[64,192]{1,0:T(8,128)(2,1)} %constant.8.clone.fi_hbm, bf16[4,512,2048]{2,1,0:T(8,128)(2,1)} %hist_hbm.1, bf16[512,2048]{1,0:T(8,128)(2,1)} %taps_hbm.1, ...), custom_call_target="tpu_custom_call" | custom-call | tf_op jit(solution)/shard_map/pallas_call | solution.py:366
  24.9 0.7 %copy.9 = bf16[4,16,2048]{2,1,0:T(8,128)(2,1)} copy(bf16[4,16,2048]{2,1,0:T(8,128)(2,1)S(1)} %shard_map.73) | data formatting | bytes 524288

commit v3 on v2

--- a/solution.py
+++ b/solution.py
@@ -14,6 +14,7 @@
 BF16 = jnp.bfloat16
 LEFT_HOP = 3
 LEFT_GAP = 5
+OTHER_LEFT_GAP = 3
 RIGHT_GAP = 0
 RIGHT_HOP = 4
 DEPTH = 2
@@ -276,7 +277,7 @@
             action(i)
 
     def turn(way, k):
-        gap = RIGHT_GAP if way == 0 else LEFT_GAP
+        gap = RIGHT_GAP if way == 0 else jnp.where(core == 0, LEFT_GAP, OTHER_LEFT_GAP)
         return gap * k + jnp.where(k == n - 2, chunks - gap, 0)
 
     left_lag = jnp.where(last, 0, LEFT_HOP * ends - 1)

time: 25.8 us -> 25.8 us (level)
  no operation moved by 1% of the time
where the time goes in v3:
time: 25.8 us; the launch traced here: 25.6 us
  Pallas kernels  24.9 us (97%)
  local copies, waits for them, and re-layouts  0.71 us (3%)
    pallas_call x1, Pallas kernels, body(): pl.pallas_call(functools.partial(kernel, n, new, piece, width), out_shape...  24.9 us
    unnamed x1, local copies, waits for them, and re-layouts  0.71 us

profile of v3, /device:TPU:0, one launch (start us, length us, event | category | flops | bytes accessed | tf_op | source)
XLA Modules:
  0.0 25.6 jit_solution(10658678994599239816)
XLA Ops:
  0.0 24.9 %shard_map.73 = bf16[4,16,2048]{2,1,0:T(8,128)(2,1)S(1)} custom-call(bf16[192,192]{1,0:T(8,128)(2,1)} %constant.6.clone.ft_hbm, bf16[192,128]{1,0:T(8,128)(2,1)} %constant.7.clone.fh_hbm, bf16[64,192]{1,0:T(8,128)(2,1)} %constant.8.clone.fi_hbm, bf16[4,512,2048]{2,1,0:T(8,128)(2,1)} %hist_hbm.1, bf16[512,2048]{1,0:T(8,128)(2,1)} %taps_hbm.1, ...), custom_call_target="tpu_custom_call" | custom-call | tf_op jit(solution)/shard_map/pallas_call | solution.py:367
  24.9 0.7 %copy.9 = bf16[4,16,2048]{2,1,0:T(8,128)(2,1)} copy(bf16[4,16,2048]{2,1,0:T(8,128)(2,1)S(1)} %shard_map.73) | data formatting | bytes 524288
